TPU v7x, 768 devices: a whole 4x8x12 slice. The times are simulated.
768 devices in a mesh: dp: 64 (over x, y, core), tensor: 12 (over z).
Axes of the slice: x: 4, y: 8, z: 12, core: 2. Of those that a mesh axis runs over, the one named last changes fastest.
Arguments:
- gradient: float32 [5120, 27648], P('dp', 'tensor'), may hold values from -6 to 6
- momentum: float32 [5120, 27648], P('dp', 'tensor'), may hold values from -6 to 6
- right_factor: float32 [27648, 256], P('tensor'), may hold values from -6 to 6
Outputs:
- update: float32 [5120, 27648], P('dp', 'tensor')
- new_momentum: float32 [5120, 27648], P('dp', 'tensor')
- new_right: float32 [27648, 256], P('tensor')
All inputs are finite; a program needn't handle non-finite values.
Results may differ from a plain program's by a relative error of at most 0.000098.
Values sent between devices are 32-bit elements; how exact they have to be, the bound alone decides.
A program may use at most 64 MiB of HBM per device.

v0:
```python
import jax
import jax.numpy as jnp
from jax import lax
from jax.sharding import Mesh
from jax.sharding import PartitionSpec as P

ROWS = 5120
COLS = 27648
RANK = 256
DP = ("dp_0", "dp_1", "dp_2")
DP_TENSOR = ("dp_0", "dp_1", "dp_2", "tensor")


def sent_to_all(value, axis):
    copies = jnp.broadcast_to(value, (lax.axis_size(axis), *value.shape))
    return lax.all_to_all(copies, axis, split_axis=0, concat_axis=0, tiled=True)


def over_copies(value, axis):
    everything = sent_to_all(value, axis)
    return jnp.sum(everything, axis=0)


def split_up(value, dim, size):
    lengths = value.shape
    blocks = value.reshape(*lengths[:dim], size, lengths[dim] // size, *lengths[dim + 1 :])
    return jnp.moveaxis(blocks, dim, 0)


def sum_at_owner(value, axis, dim):
    blocks = split_up(value, dim, lax.axis_size(axis))
    arrived = lax.all_to_all(blocks, axis, split_axis=0, concat_axis=0, tiled=True)
    return arrived.sum(axis=0)


def over_axes(value, axes):
    for axis in axes:
        value = lax.psum(value, axis)
    return value


def laid_out(blocks, dim):
    lengths = list(blocks.shape[1:])
    lengths[dim] *= blocks.shape[0]
    return jnp.moveaxis(blocks, 0, dim).reshape(lengths)


def gathered_copies(value, axis, dim):
    return laid_out(sent_to_all(value, axis), dim)


def on_device(gradient, momentum, right_factor):
    high = lax.Precision.HIGHEST
    buffer = momentum + gradient
    partial_value = jnp.dot(
        buffer, right_factor, precision=high, preferred_element_type=jnp.float32
    )
    left = over_copies(partial_value, "tensor")
    gram = lax.psum(jnp.dot(left.T, left, precision=high, preferred_element_type=jnp.float32), DP)
    chol = jnp.linalg.cholesky(gram)
    ortho = jax.scipy.linalg.solve_triangular(chol, left.T, lower=True).T
    owned = sum_at_owner(
        jnp.dot(buffer.T, ortho, precision=high, preferred_element_type=jnp.float32), DP, 0
    )
    squares = over_axes(jnp.sum(owned * owned, axis=0), DP_TENSOR)
    scale_col = jnp.sqrt(squares / COLS + 1e-06)
    new_right = gathered_copies(owned / scale_col, DP, 0)
    right = new_right * scale_col
    new_momentum = buffer - 0.05 * jnp.dot(
        ortho, right.T, precision=high, preferred_element_type=jnp.float32
    )
    factor = (ROWS / RANK) ** 0.5
    update = factor * jnp.dot(
        ortho, new_right.T, precision=high, preferred_element_type=jnp.float32
    )
    return (update, new_momentum, new_right)


def solution(mesh):
    finer = Mesh(
        mesh.devices.reshape(4, 8, 2, mesh.shape["tensor"]), ("dp_0", "dp_1", "dp_2", "tensor")
    )
    placed = (P(DP, "tensor"), P(DP, "tensor"), P("tensor", None))
    return jax.shard_map(
        on_device,
        mesh=finer,
        in_specs=placed,
        out_specs=(P(DP, "tensor"), P(DP, "tensor"), P("tensor", None)),
        check_vma=False,
    )
```

profile of v0, /device:TPU:1, one launch (start us, length us, event | category | flops | bytes accessed | tf_op | source)
XLA Modules:
  0.0 552.9 jit_solution(7261923146568410227)
XLA Ops:
  7.2 0.0 copy-start
  7.2 0.0 all-reduce.3.cloned.1.call-start
  7.2 1.6 add.42
  8.8 0.5 copy-done
  9.3 1.3 fusion.16
  10.6 0.1 broadcast_in_dim.10
  10.7 53.6 %all_to_all.15 = f32[12,80,256]{2,1,0:T(8,128)} all-to-all(f32[12,80,256]{2,1,0:T(8,128)S(1)} %broadcast_in_dim.10), channel_id=1, replica_groups=mesh['dp_0'=4,'dp_1'=8,'dp_2'=2,'tensor'=12] {'tensor'}, dimensions={0} | all-to-all | bytes 1966080 | tf_op jit(solution)/shard_map/all_to_all | solution.py:16
  64.3 1.3 reduce_sum.27
  65.5 1.1 fusion.17
  66.7 0.0 all-reduce.3.cloned.1.call-update
  66.7 196.5 %all-reduce.3.cloned.1.call-done = f32[256,256]{0,1:T(8,128)} async-done(((f32[256,256]{0,1:T(8,128)}), f32[256,256]{0,1:T(8,128)}) %all-reduce.3.cloned.1.call-update) | async-done | bytes 262160 | tf_op jit(solution)/shard_map/psum | solution.py:59
  263.2 1.1 copy.11
  264.3 1.0 fusion.3
  265.3 0.0 copy-start.3
  265.3 0.7 copy-done.3
  266.0 11.7 %cholesky.50 = f32[128,128]{1,0:T(8,128)S(1)} custom-call(f32[128,128]{1,0:T(8,128)S(1)} %cholesky.118), custom_call_target="Cholesky" | custom-call | tf_op jit(solution)/shard_map/jit(cholesky)/cholesky | solution.py:60
  277.7 0.7 select_reduce_fusion.1
  278.4 10.6 %custom-call.15 = f32[1,128,128]{1,2,0:T(8,128)S(1)} custom-call(f32[1,128,128]{2,1,0:T(8,128)} %get-tuple-element.24), custom_call_target="InvertDiagBlocksLowerTriangular" | custom-call | tf_op jit(solution)/shard_map/jit(cholesky)/cholesky | solution.py:60
  289.1 1.0 constant_dynamic-update-slice_fusion.1
  290.1 1.7 convolution_subtract_fusion
  291.9 12.5 %cholesky.105 = f32[128,128]{1,0:T(8,128)S(1)} custom-call(f32[128,128]{1,0:T(8,128)} %convolution_subtract_fusion), custom_call_target="Cholesky" | custom-call | tf_op jit(solution)/shard_map/jit(cholesky)/cholesky | solution.py:60
  304.5 0.0 copy-start.2
  304.5 0.7 compare_reduce_fusion
  306.5 0.0 copy-done.2
  306.5 1.0 select_select_fusion
  307.5 0.1 triangular_solve.57
  307.6 5.2 while.1
  307.6 0.6 fusion.29
  308.2 2.0 bitcast_dynamic-update-slice_fusion.2
  310.2 0.6 fusion.29
  310.8 2.0 bitcast_dynamic-update-slice_fusion.2
  312.8 21.1 %custom-call.16 = f32[2,128,128]{1,2,0:T(8,128)} custom-call(f32[2,128,128]{2,1,0:T(8,128)} %get-tuple-element.10), custom_call_target="InvertDiagBlocksLowerTriangular" | custom-call | tf_op jit(solution)/shard_map/jit(_solve_triangular)/triangular_solve | solution.py:61
  333.9 1.0 fusion.6
  334.9 0.2 convolution_subtract_fusion.1
  335.2 1.0 fusion.5
  336.2 3.5 fusion.10
  339.7 3.3 reshape.32
  343.0 68.8 %all_to_all.16 = f32[64,36,256]{2,1,0:T(8,128)} all-to-all(f32[64,36,256]{2,1,0:T(8,128)} %reshape.32), channel_id=1, replica_groups=mesh['dp_0'=4,'dp_1'=8,'dp_2'=2,'tensor'=12] {'dp_0','dp_1','dp_2'}, dimensions={0} | all-to-all | bytes 4718592 | tf_op jit(solution)/shard_map/all_to_all | solution.py:32
  411.8 1.9 reduce_sum.28
  413.8 8.7 %psum.36 = f32[256]{0:T(256)S(1)} all-reduce(f32[256]{0:T(256)S(1)} %multiply_reduce_fusion), channel_id=1, replica_groups=mesh['dp_0'=4,'dp_1'=8,'dp_2'=2,'tensor'=12] {'dp_0'}, use_global_device_ids=true, to_apply=%region_8.9 | all-reduce | flops 256 | bytes 2048 | tf_op jit(solution)/shard_map/psum | solution.py:38
  422.4 11.0 %psum.37 = f32[256]{0:T(256)S(1)} all-reduce(f32[256]{0:T(256)S(1)} %psum.36), channel_id=1, replica_groups=mesh['dp_0'=4,'dp_1'=8,'dp_2'=2,'tensor'=12] {'dp_1'}, use_global_device_ids=true, to_apply=%region_9.10 | all-reduce | flops 256 | bytes 2048 | tf_op jit(solution)/shard_map/psum | solution.py:38
  433.4 8.2 %psum.38 = f32[256]{0:T(256)S(1)} all-reduce(f32[256]{0:T(256)S(1)} %psum.37), channel_id=1, replica_groups=mesh['dp_0'=4,'dp_1'=8,'dp_2'=2,'tensor'=12] {'dp_2'}, use_global_device_ids=true, to_apply=%region_10.11 | all-reduce | flops 256 | bytes 2048 | tf_op jit(solution)/shard_map/psum | solution.py:38
  441.6 19.9 %psum.39 = f32[256]{0:T(256)S(1)} all-reduce(f32[256]{0:T(256)S(1)} %psum.38), channel_id=1, replica_groups=mesh['dp_0'=4,'dp_1'=8,'dp_2'=2,'tensor'=12] {'tensor'}, use_global_device_ids=true, to_apply=%region_11.12 | all-reduce | flops 256 | bytes 2048 | tf_op jit(solution)/shard_map/psum | solution.py:38
  461.6 0.2 broadcast_in_dim.11
  461.7 72.7 %all_to_all.17 = f32[64,36,256]{2,1,0:T(8,128)} all-to-all(f32[64,36,256]{2,1,0:T(8,128)S(1)} %broadcast_in_dim.11), channel_id=1, replica_groups=mesh['dp_0'=4,'dp_1'=8,'dp_2'=2,'tensor'=12] {'dp_0','dp_1','dp_2'}, dimensions={0} | all-to-all | bytes 4718592 | tf_op jit(solution)/shard_map/all_to_all | solution.py:16
  534.4 3.4 reshape.33
  537.8 0.0 copy-start.1
  537.8 5.0 fusion
  542.8 0.0 copy-done.1
  542.8 3.3 convolution_multiply_fusion.1
  (10 shorter events, 0.1 us)
Async XLA Ops:
  7.2 2.1 copy-start
  7.2 256.1 %all-reduce.3.cloned.1.call-start = ((), (), s32[]{:S(2)}) async-start(), calls=%async_computation.3 | async-start | bytes 524288 | tf_op jit(solution)/shard_map/psum | solution.py:59
  265.3 0.7 copy-start.3
  304.5 2.1 copy-start.2
  537.8 5.0 copy-start.1
Sparse Core Ops, SparseCore 0:
  66.8 196.4 all-reduce.2
where the time goes:
time: 554 us; the launch traced here: 553 us
  blocking collectives  243 us (44%)
  waiting for transfers between devices  197 us (36%)
  other arithmetic  64.2 us (12%)
  matrix products  19.2 us (3%)
  between operations  15.5 us (3%)
  local copies, waits for them, and re-layouts  14.6 us (3%)
    psum x1, waiting for transfers between devices, on_device(): lax.psum(jnp.dot(left.T, left, precision=high, preferred_element_type=jnp...  197 us
    all_to_all x2, blocking collectives, sent_to_all(): return lax.all_to_all(copies, axis, split_axis=0, concat_axis=0, tiled=True)  126 us
    all_to_all x1, blocking collectives, sum_at_owner(): lax.all_to_all(blocks, axis, split_axis=0, concat_axis=0, tiled=True)  68.8 us
    psum x4, blocking collectives, over_axes(): value = lax.psum(value, axis)  47.8 us
    another operation x6, other arithmetic, on_device(): chol = jnp.linalg.cholesky(gram)  36.3 us
    another operation x3, other arithmetic, on_device(): ortho = jax.scipy.linalg.solve_triangular(chol, left.T, lower=True).T  22.1 us
  transfers between devices with their start and end apart: 1, of which 1 were waited for; matrix products, arithmetic and copies ran while one was open for 0% of the time, Pallas kernels for 0%

commit v1 on v0

v1 whole, which is shorter than its diff:
```python
import jax
import jax.numpy as jnp
from jax import lax
from jax.experimental import pallas as pl
from jax.experimental.pallas import tpu as pltpu
from jax.sharding import Mesh
from jax.sharding import PartitionSpec as P

ROWS = 5120
COLS = 27648
RANK = 256
NX, NY, NC, NZ = 4, 8, 2, 12
DP = ("dp_0", "dp_1", "dp_2")
HIGH = lax.Precision.HIGHEST
F32 = jnp.float32
MESH = pl.DeviceIdType.MESH
LOCAL_ROWS = ROWS // (NX * NY * NC)
LOCAL_COLS = COLS // NZ
BLOCKS = LOCAL_COLS // 256
X_FIRST = 6
Y_FIRST = BLOCKS - X_FIRST
XW, YW = 128 * X_FIRST, 128 * Y_FIRST
PANEL = 64


def dot(a, b, dims=((1,), (0,))):
    return lax.dot_general(a, b, (dims, ((), ())), precision=HIGH, preferred_element_type=F32)


def eliminate_slab(ws, p, s):
    r0 = PANEL * p + 8 * s
    end = PANEL * (p + 1)
    n = end - r0
    lo = (r0 // 128) * 128
    hi = RANK + (r0 // 128 + 1) * 128
    cols = [jnp.broadcast_to(ws[r0:end, r0 + j : r0 + j + 1], (n, 128)) for j in range(8)]
    w = ws[r0:end, lo:hi]
    sub = lax.broadcasted_iota(jnp.int32, (n, 128), 0)
    wide_sub = lax.broadcasted_iota(jnp.int32, w.shape, 0)
    reps = (hi - lo) // 128
    for j in range(8):
        rs = lax.rsqrt(cols[j][j : j + 1, :])
        l = cols[j] * rs
        for m in range(j + 1, 8):
            cols[m] = cols[m] - l * l[m : m + 1, :]
        lm = jnp.concatenate([jnp.where(sub > j, l, 0.0)] * reps, axis=1)
        u = w[j : j + 1, :] * jnp.concatenate([rs] * reps, axis=1)
        w = jnp.where(wide_sub == j, jnp.broadcast_to(u, w.shape), w - lm * u)
    ws[r0:end, lo:hi] = w


def update_below(ws, p):
    a, b = PANEL * p, PANEL * (p + 1)
    lo = (b // 128) * 128
    hi = RANK + ((b - 1) // 128 + 1) * 128
    full = dot(ws[a:b, lo:RANK], ws[a:b, lo:hi], ((0,), (0,)))
    ws[b:RANK, lo:hi] = ws[b:RANK, lo:hi] - full[b - lo :, :]


def factor_panel(ws, p):
    for s in range(PANEL // 8):
        eliminate_slab(ws, p, s)
    if PANEL * (p + 1) < RANK:
        update_below(ws, p)


def offsets(n):
    return sorted(range(1, n), key=lambda off: -min(off, n - off))


def main_kernel(
    g_ref, m_ref, r_ref, rt_ref, ortho_ref, inv_ref,
    bbuf, pbuf, pin, lbuf, lt, gp, gpin, gyin, gxs, gfull, ws,
    mx, my, mxin, myin, xin1, xs, xin2, yin1, ys, yin2, fx, fy, sq,
    pa_s, pa_r, lb_s, lb_r, pr_s, pr_r, gy_s, gy_r, gx_s, gx_r, ga_s, ga_r, gd_s, gd_r,
    x1_s, x1_r, x2_s, x2_r, y1_s, y1_r, y2_s, y2_r,
    ax1_s, ax1_r, ax2_s, ax2_r, ay1_s, ay1_r, ay2_s, ay2_r, dd_s, dd_r, sq_s, sq_r,
):
    x, y, c, z = (lax.axis_index(a) for a in (*DP, "tensor"))
    other = 1 - c

    def at_x(off):
        return lax.rem(x + off, NX)

    def at_y(off):
        return lax.rem(y + off, NY)

    def at_z(off):
        return lax.rem(z + off, NZ)

    def send(src, dst, s, r, where):
        copy = pltpu.make_async_remote_copy(
            src_ref=src, dst_ref=dst, send_sem=s, recv_sem=r, device_id=where, device_id_type=MESH
        )
        copy.start()
        return copy

    barrier = pltpu.get_barrier_semaphore()
    greet = [{"tensor": at_z(o)} for o in range(1, NZ)]
    greet += [{"dp_1": at_y(o)} for o in range(1, NY)]
    greet += [{"dp_0": at_x(o)} for o in range(1, NX)]
    greet += [{"dp_2": other}]
    for where in greet:
        pl.semaphore_signal(barrier, inc=1, device_id=where, device_id_type=MESH)

    pending = []

    b = g_ref[...] + m_ref[...]
    bbuf[0:LOCAL_ROWS, :] = b
    bbuf[LOCAL_ROWS:128, :] = jnp.zeros((128 - LOCAL_ROWS, LOCAL_COLS), F32)
    part = dot(bbuf[0:LOCAL_ROWS, :], r_ref[...])
    for i in range(NZ):
        if 8 * i < LOCAL_ROWS:
            pbuf[i] = part[8 * i : 8 * i + 8, :]
        else:
            pbuf[i] = jnp.zeros((8, RANK), F32)
    pl.semaphore_wait(barrier, len(greet))

    copies = {}
    for o in offsets(NZ):
        to = at_z(o)
        copies[o] = send(pbuf.at[to], pin.at[o - 1], pa_s.at[o - 1], pa_r.at[o - 1], {"tensor": to})
    total = pbuf[z]
    for o in range(1, NZ):
        copies[o].wait_recv()
        total = total + pin[o - 1]
    pending += copies.values()
    lbuf[z] = total
    copies = {}
    for o in offsets(NZ):
        copies[o] = send(lbuf.at[z], lbuf.at[z], lb_s.at[o - 1], lb_r.at[o - 1], {"tensor": at_z(o)})
    for o in range(1, NZ):
        copies[o].wait_recv()
    pending += copies.values()

    left = jnp.concatenate([lbuf[i] for i in range(LOCAL_ROWS // 8)] + [jnp.zeros((128 - LOCAL_ROWS, RANK), F32)], axis=0)
    lt[...] = left.T

    gram = dot(lt[...], left)
    for h in range(NC):
        for i in range(NY):
            gp[h, i] = gram[128 * h + 16 * i : 128 * h + 16 * i + 16, :]
    pair = {"dp_2": other}
    g_pair = send(gp.at[other], gpin, pr_s.at[0], pr_r.at[0], pair)

    def products(h):
        rows = lt[pl.ds(pl.multiple_of(128 * h, 128), 128), :]
        for t in range(BLOCKS):
            d = dot(rows, bbuf[:, 256 * t : 256 * t + 256])
            for i in range(NY):
                for q in range(2):
                    for k in range(2):
                        piece = d[16 * i + 8 * q : 16 * i + 8 * q + 8, 128 * k : 128 * k + 128]
                        if t < X_FIRST:
                            mx[h, 2 * q + k, i, :, 128 * t : 128 * t + 128] = piece
                        else:
                            my[h, 2 * q + k, i, :, 128 * (t - X_FIRST) : 128 * (t - X_FIRST) + 128] = piece

    products(other)
    y_pair = send(my.at[other], myin, pr_s.at[1], pr_r.at[1], pair)
    x_pair = send(mx.at[other], mxin, pr_s.at[2], pr_r.at[2], pair)

    g_pair.wait_recv()
    for i in range(NY):
        gp[c, i] = gp[c, i] + gpin[i]
    copies_g = {}
    for o in offsets(NY):
        to = at_y(o)
        copies_g[o] = send(gp.at[c, to], gyin.at[o - 1], gy_s.at[o - 1], gy_r.at[o - 1], {"dp_1": to})

    products(c)
    y_pair.wait_recv()
    for i in range(NX):
        my[c, i] = my[c, i] + myin[i]
    copies_y1 = {}
    for o in offsets(NY):
        to = at_y(o)
        copies_y1[o] = send(my.at[c, :, to], yin1.at[o - 1], y1_s.at[o - 1], y1_r.at[o - 1], {"dp_1": to})
    x_pair.wait_recv()
    for i in range(NX):
        mx[c, i] = mx[c, i] + mxin[i]
    copies_x1 = {}
    for o in offsets(NX):
        to = at_x(o)
        copies_x1[o] = send(mx.at[c, to], xin1.at[o - 1], x1_s.at[o - 1], x1_r.at[o - 1], {"dp_0": to})
    pending += [g_pair, y_pair, x_pair, *copies_g.values(), *copies_y1.values(), *copies_x1.values()]

    total = gp[c, y]
    for o in range(1, NY):
        copies_g[o].wait_recv()
        total = total + gyin[o - 1]
    gxs[x] = total
    copies = {}
    for o in offsets(NX):
        copies[o] = send(gxs.at[x], gxs.at[x], gx_s.at[o - 1], gx_r.at[o - 1], {"dp_0": at_x(o)})
    pending += copies.values()

    for o in range(1, NY):
        copies_y1[o].wait_recv()
    for i in range(NX):
        acc = my[c, i, y]
        for o in range(1, NY):
            acc = acc + yin1[o - 1, i]
        ys[i] = acc
    copies_y2 = {}
    for o in offsets(NX):
        to = at_x(o)
        copies_y2[o] = send(ys.at[to], yin2.at[o - 1], y2_s.at[o - 1], y2_r.at[o - 1], {"dp_0": to})
    pending += copies_y2.values()

    for o in range(1, NX):
        copies[o].wait_recv()
    total = gxs[0]
    for i in range(1, NX):
        total = total + gxs[i]
    gfull[c, y] = total
    copies_ga = {}
    for o in offsets(NY):
        copies_ga[o] = send(gfull.at[c, y], gfull.at[c, y], ga_s.at[o - 1], ga_r.at[o - 1], {"dp_1": at_y(o)})
    pending += copies_ga.values()

    for o in range(1, NX):
        copies_x1[o].wait_recv()
    for i in range(NY):
        acc = mx[c, x, i]
        for o in range(1, NX):
            acc = acc + xin1[o - 1, i]
        xs[i] = acc
    copies_x2 = {}
    for o in offsets(NY):
        to = at_y(o)
        copies_x2[o] = send(xs.at[to], xin2.at[o - 1], x2_s.at[o - 1], x2_r.at[o - 1], {"dp_1": to})
    pending += copies_x2.values()

    for o in range(1, NY):
        copies_ga[o].wait_recv()
    g_both = send(gfull.at[c], gfull.at[c], gd_s, gd_r, pair)
    pending += [g_both]

    acc = ys[x]
    for o in range(1, NX):
        copies_y2[o].wait_recv()
        acc = acc + yin2[o - 1]
    fy[c, x, y] = acc
    back_y1 = {}
    for o in offsets(NX):
        back_y1[o] = send(fy.at[c, x, y], fy.at[c, x, y], ay1_s.at[o - 1], ay1_r.at[o - 1], {"dp_0": at_x(o)})
    pending += back_y1.values()

    g_both.wait_recv()
    for h in range(NC):
        for i in range(NY):
            r0 = 128 * h + 16 * i
            ws[r0 : r0 + 16, 0:RANK] = gfull[h, i]
    ri = lax.broadcasted_iota(jnp.int32, (RANK, RANK), 0)
    ci = lax.broadcasted_iota(jnp.int32, (RANK, RANK), 1)
    ws[:, RANK:] = jnp.where(ri == ci, 1.0, 0.0)

    acc = xs[y]
    for o in range(1, NY):
        copies_x2[o].wait_recv()
        acc = acc + xin2[o - 1]
    fx[c, x, y] = acc
    back_x1 = {}
    for o in offsets(NY):
        back_x1[o] = send(fx.at[c, x, y], fx.at[c, x, y], ax1_s.at[o - 1], ax1_r.at[o - 1], {"dp_1": at_y(o)})
    pending += back_x1.values()

    factor_panel(ws, 0)

    for o in range(1, NX):
        back_y1[o].wait_recv()
    back_y2 = {}
    for o in offsets(NY):
        back_y2[o] = send(fy.at[c, :, y], fy.at[c, :, y], ay2_s.at[o - 1], ay2_r.at[o - 1], {"dp_1": at_y(o)})
    pending += back_y2.values()

    factor_panel(ws, 1)

    for o in range(1, NY):
        back_x1[o].wait_recv()
    back_x2 = {}
    for o in offsets(NX):
        back_x2[o] = send(fx.at[c, x], fx.at[c, x], ax2_s.at[o - 1], ax2_r.at[o - 1], {"dp_0": at_x(o)})
    pending += back_x2.values()

    factor_panel(ws, 2)
    factor_panel(ws, 3)
    inverse = ws[:, RANK:]
    ortho_ref[...] = dot(left[0:LOCAL_ROWS, :], inverse, ((1,), (1,)))

    for o in range(1, NY):
        back_y2[o].wait_recv()
    y_both = send(fy.at[c], fy.at[c], dd_s.at[0], dd_r.at[0], pair)
    for o in range(1, NX):
        back_x2[o].wait_recv()
    x_both = send(fx.at[c], fx.at[c], dd_s.at[1], dd_r.at[1], pair)
    pending += [y_both, x_both]
    y_both.wait_recv()
    x_both.wait_recv()

    inverse = ws[:, RANK:]
    acc = jnp.zeros((RANK, 128), F32)
    for t in range(BLOCKS):
        src, t0 = (fx, t) if t < X_FIRST else (fy, t - X_FIRST)
        halves = []
        for k in range(2):
            halves.append(
                jnp.concatenate(
                    [src[h, 2 * q + k, i, :, 128 * t0 : 128 * t0 + 128] for h in range(NC) for i in range(NY) for q in range(2)],
                    axis=0,
                )
            )
        d = dot(inverse, jnp.concatenate(halves, axis=1))
        rt_ref[:, 256 * t : 256 * t + 256] = d
        acc = acc + d[:, 0:128] * d[:, 0:128] + d[:, 128:256] * d[:, 128:256]
    sq[z] = jnp.sum(acc.T, axis=0, keepdims=True)
    copies = {}
    for o in offsets(NZ):
        copies[o] = send(sq.at[z], sq.at[z], sq_s.at[o - 1], sq_r.at[o - 1], {"tensor": at_z(o)})
    pending += copies.values()
    for o in range(1, NZ):
        copies[o].wait_recv()
    total = sq[0]
    for i in range(1, NZ):
        total = total + sq[i]
    inv_ref[...] = 1.0 / jnp.sqrt(total / COLS + 1e-06)

    for copy in pending:
        copy.wait_send()


def final_kernel(g_ref, m_ref, rt_ref, ortho_ref, inv_ref, up_ref, nm_ref, nr_ref):
    ortho = ortho_ref[...]
    inv = inv_ref[...]
    rt = rt_ref[...]
    nm_ref[...] = (g_ref[...] + m_ref[...]) - 0.05 * dot(ortho, rt)
    up_ref[...] = dot(ortho * (inv * ((ROWS / RANK) ** 0.5)), rt)
    nr_ref[...] = rt.T * inv


def on_device(gradient, momentum, right_factor):
    vmem = pl.BlockSpec(memory_space=pltpu.VMEM)
    dma = pltpu.SemaphoreType.DMA
    v = lambda *shape: pltpu.VMEM(shape, F32)
    rt, ortho, inv = pl.pallas_call(
        main_kernel,
        name="sums",
        out_shape=(
            jax.ShapeDtypeStruct((RANK, LOCAL_COLS), F32),
            jax.ShapeDtypeStruct((LOCAL_ROWS, RANK), F32),
            jax.ShapeDtypeStruct((1, RANK), F32),
        ),
        in_specs=[vmem] * 3,
        out_specs=[vmem] * 3,
        scratch_shapes=[
            v(128, LOCAL_COLS), v(NZ, 8, RANK), v(NZ - 1, 8, RANK), v(NZ, 8, RANK), v(RANK, 128),
            v(NC, NY, 16, RANK), v(NY, 16, RANK), v(NY - 1, 16, RANK), v(NX, 16, RANK), v(NC, NY, 16, RANK), v(RANK, 2 * RANK),
            v(NC, NX, NY, 8, XW), v(NC, NX, NY, 8, YW), v(NX, NY, 8, XW), v(NX, NY, 8, YW),
            v(NX - 1, NY, 8, XW), v(NY, 8, XW), v(NY - 1, 8, XW),
            v(NY - 1, NX, 8, YW), v(NX, 8, YW), v(NX - 1, 8, YW),
            v(NC, NX, NY, 8, XW), v(NC, NX, NY, 8, YW), v(NZ, 1, RANK),
            dma((NZ - 1,)), dma((NZ - 1,)), dma((NZ - 1,)), dma((NZ - 1,)), dma((3,)), dma((3,)),
            dma((NY - 1,)), dma((NY - 1,)), dma((NX - 1,)), dma((NX - 1,)), dma((NY - 1,)), dma((NY - 1,)), dma, dma,
            dma((NX - 1,)), dma((NX - 1,)), dma((NY - 1,)), dma((NY - 1,)),
            dma((NY - 1,)), dma((NY - 1,)), dma((NX - 1,)), dma((NX - 1,)),
            dma((NY - 1,)), dma((NY - 1,)), dma((NX - 1,)), dma((NX - 1,)),
            dma((NX - 1,)), dma((NX - 1,)), dma((NY - 1,)), dma((NY - 1,)),
            dma((2,)), dma((2,)), dma((NZ - 1,)), dma((NZ - 1,)),
        ],
        compiler_params=pltpu.CompilerParams(
            collective_id=0, has_side_effects=True, vmem_limit_bytes=62 * 2**20
        ),
    )(gradient, momentum, right_factor)
    steps = 3
    width = LOCAL_COLS // steps
    wide = pl.BlockSpec((LOCAL_ROWS, width), lambda i: (0, i))
    return tuple(
        pl.pallas_call(
            final_kernel,
            name="outputs",
            grid=(steps,),
            out_shape=(
                jax.ShapeDtypeStruct((LOCAL_ROWS, LOCAL_COLS), F32),
                jax.ShapeDtypeStruct((LOCAL_ROWS, LOCAL_COLS), F32),
                jax.ShapeDtypeStruct((LOCAL_COLS, RANK), F32),
            ),
            in_specs=[
                wide, wide, pl.BlockSpec((RANK, width), lambda i: (0, i)),
                pl.BlockSpec((LOCAL_ROWS, RANK), lambda i: (0, 0)), pl.BlockSpec((1, RANK), lambda i: (0, 0)),
            ],
            out_specs=[wide, wide, pl.BlockSpec((width, RANK), lambda i: (i, 0))],
        )(gradient, momentum, rt, ortho, inv)
    )


def solution(mesh):
    finer = Mesh(mesh.devices.reshape(NX, NY, NC, mesh.shape["tensor"]), (*DP, "tensor"))
    return jax.shard_map(
        on_device,
        mesh=finer,
        in_specs=(P(DP, "tensor"), P(DP, "tensor"), P("tensor", None)),
        out_specs=(P(DP, "tensor"), P(DP, "tensor"), P("tensor", None)),
        check_vma=False,
    )
```

time: 554 us -> 104 us (0.19)
  blocking collectives: 243 us -> 0 us
  waiting for transfers between devices: 197 us -> 0 us
  Pallas kernels: 0 us -> 103 us
  other arithmetic: 64.2 us -> 0 us
  matrix products: 19.2 us -> 0 us
  between operations: 15.5 us -> 0.64 us
  local copies, waits for them, and re-layouts: 14.6 us -> 0 us
    psum x1 -> x0, waiting for transfers between devices: 197 us -> none  [on_device(): lax.psum(jnp.dot(left.T, left, precision=high, preferred_element_type=jnp...]
    all_to_all x3 -> x0, blocking collectives: 195 us -> none  [the longest x2 126 us: sent_to_all(): return lax.all_to_all(copies, axis, split_axis=0, concat_axis=0, tiled=True)]
    pallas_call x0 -> x2, Pallas kernels: none -> 103 us  [the longest x1 96.6 us: on_device(): pl.pallas_call(main_kernel, name='sums', out_shape=(jax.ShapeDtypeStruct(...]
    another operation x9 -> x0, other arithmetic: 58.4 us -> none  [the longest x6 36.3 us: on_device(): chol = jnp.linalg.cholesky(gram)]
    psum x4 -> x0, blocking collectives: 47.8 us -> none  [over_axes(): value = lax.psum(value, axis)]
    dot_general x5 -> x0, matrix products: 14.1 us -> none  [the longest x1 4.97 us: on_device(): jnp.dot(ortho, right.T, precision=high, preferred_element_type=jnp.float32)]
    reshape x2 -> x0, local copies, waits for them, and re-layouts: 6.71 us -> none  [the longest x1 3.39 us: laid_out(): return jnp.moveaxis(blocks, 0, dim).reshape(lengths)]
  transfers between devices with their start and end apart: 1 -> 0, of which waited for: 1 -> 0; matrix products, arithmetic and copies ran while one was open for 0% -> 0% of each run, Pallas kernels for 0% -> 0%
where the time goes in v1:
time: 104 us; the launch traced here: 103 us
  Pallas kernels  103 us (99%)
    pallas_call x1, Pallas kernels, on_device(): pl.pallas_call(main_kernel, name='sums', out_shape=(jax.ShapeDtypeStruct(...  96.6 us
    pallas_call x1, Pallas kernels, on_device(): pl.pallas_call(final_kernel, name='outputs', grid=(steps,), out_shape=(ja...  6.26 us

profile of v1, /device:TPU:1, one launch (start us, length us, event | category | flops | bytes accessed | tf_op | source)
XLA Modules:
  0.0 103.5 jit_solution(5199512110959842987)
XLA Ops:
  0.6 96.6 %sums.1 = (f32[256,2304]{1,0:T(8,128)}, f32[80,256]{1,0:T(8,128)}, f32[1,256]{1,0:T(1,128)}) custom-call(f32[80,2304]{1,0:T(8,128)} %g_ref.3, f32[80,2304]{1,0:T(8,128)} %m_ref.3, f32[2304,256]{1,0:T(8,128)} %r_ref.1), custom_call_target="tpu_custom_call" | custom-call | tf_op jit(solution)/shard_map/sums/pallas_call | solution.py:346
  97.2 6.3 %outputs.1 = (f32[80,2304]{1,0:T(8,128)}, f32[80,2304]{1,0:T(8,128)}, f32[2304,256]{1,0:T(8,128)}) custom-call(f32[80,2304]{1,0:T(8,128)} %g_ref.3, f32[80,2304]{1,0:T(8,128)} %m_ref.3, f32[256,2304]{1,0:T(8,128)} %get-tuple-element.6.rt_ref, f32[80,256]{1,0:T(8,128)} %get-tuple-element.7.ortho_ref, f32[1,256]{1,0:T(1,128)} %get-tuple-element.8.inv_ref), custom_call_target="tpu_custom_call" | custom-call | tf_op jit(solution)/shard_map/outputs/pallas_call | solution.py:379

commit v2 on v0

v2 whole, which is shorter than its diff:
```python
import jax
import jax.numpy as jnp
from jax import lax
from jax.experimental import pallas as pl
from jax.experimental.pallas import tpu as pltpu
from jax.sharding import Mesh
from jax.sharding import PartitionSpec as P

ROWS = 5120
COLS = 27648
RANK = 256
NX, NY, NC, NZ = 4, 8, 2, 12
DP = ("dp_0", "dp_1", "dp_2")
HIGH = lax.Precision.HIGHEST
F32 = jnp.float32
BF16 = jnp.bfloat16
MESH = pl.DeviceIdType.MESH
LOCAL_ROWS = ROWS // (NX * NY * NC)
LOCAL_COLS = COLS // NZ
CHIP_ROWS = NC * LOCAL_ROWS
LEFT_CHUNKS = LOCAL_ROWS // 8
XS, YB = 3, 3
Y0 = 512 * XS
FETCH = 3
PANEL = 64


def dot(a, b, dims=((1,), (0,))):
    return lax.dot_general(a, b, (dims, ((), ())), precision=HIGH, preferred_element_type=F32)


def eliminate_slab(ws, p, s):
    r0 = PANEL * p + 8 * s
    end = PANEL * (p + 1)
    n = end - r0
    lo = (r0 // 128) * 128
    hi = RANK + (r0 // 128 + 1) * 128
    cols = [jnp.broadcast_to(ws[r0:end, r0 + j : r0 + j + 1], (n, 128)) for j in range(8)]
    w = ws[r0:end, lo:hi]
    sub = lax.broadcasted_iota(jnp.int32, (n, 128), 0)
    wide_sub = lax.broadcasted_iota(jnp.int32, w.shape, 0)
    reps = (hi - lo) // 128
    for j in range(8):
        rs = lax.rsqrt(cols[j][j : j + 1, :])
        l = cols[j] * rs
        for m in range(j + 1, 8):
            cols[m] = cols[m] - l * l[m : m + 1, :]
        lm = jnp.concatenate([jnp.where(sub > j, l, 0.0)] * reps, axis=1)
        u = w[j : j + 1, :] * jnp.concatenate([rs] * reps, axis=1)
        w = jnp.where(wide_sub == j, jnp.broadcast_to(u, w.shape), w - lm * u)
    ws[r0:end, lo:hi] = w


def update_below(ws, p):
    a, b = PANEL * p, PANEL * (p + 1)
    lo = (b // 128) * 128
    hi = RANK + ((b - 1) // 128 + 1) * 128
    full = dot(ws[a:b, lo:RANK], ws[a:b, lo:hi], ((0,), (0,)))
    ws[b:RANK, lo:hi] = ws[b:RANK, lo:hi] - full[b - lo :, :]


def factor_panel(ws, p):
    for s in range(PANEL // 8):
        eliminate_slab(ws, p, s)
    if PANEL * (p + 1) < RANK:
        update_below(ws, p)


def offsets(n):
    return sorted(range(1, n), key=lambda off: -min(off, n - off))


BUFFERS = dict(
    gbuf=(LOCAL_ROWS, LOCAL_COLS),
    mbuf=(LOCAL_ROWS, LOCAL_COLS),
    rfac=(LOCAL_COLS, RANK),
    bb=(CHIP_ROWS, LOCAL_COLS),
    pbuf=(NZ, 8, RANK),
    pin=(NZ - 1, 8, RANK),
    lbuf=(NZ, 8, RANK),
    lpin=(LEFT_CHUNKS, 8, RANK),
    lt=(RANK, CHIP_ROWS),
    gp=(NX, NY, 8, 128),
    gxin=(NX - 1, NY, 8, 128),
    gxs=(NY, 8, 128),
    gyin=(NY - 1, 8, 128),
    gfull=(NC, NX, NY, 8, 128),
    ws=(RANK, 2 * RANK),
    mx=(XS, NX, NY, 16, 128),
    my=(YB, NX, NY, 8, 128),
    x1in=(XS, NX - 1, NY, 16, 128),
    xs=(XS, NY, 16, 128),
    y2in=(XS, NY - 1, 16, 128),
    y1in=(YB, NY - 1, NX, 8, 128),
    ys=(NX, YB, 8, 128),
    x2in=(NX - 1, YB, 8, 128),
    fx=(NC, XS, NX, NY, 16, 128),
    fy=(NC, YB, NX, NY, 8, 128),
    rv=(LOCAL_COLS, RANK),
    sq=(NZ, 1, RANK),
)
REMOTE = dict(
    swap=(2,),
    a1=(NZ - 1,),
    a2=(NZ - 1,),
    g1=(NX - 1,),
    g2=(NY - 1,),
    g3=(NY - 1,),
    g4=(NX - 1,),
    g5=(1,),
    x1=(XS, NX - 1),
    y2=(XS, NY - 1),
    y1=(YB, NY - 1),
    x2=(NX - 1,),
    bx1=(XS, NY - 1),
    bx2=(XS, NX - 1),
    bx3=(XS,),
    by1=(NX - 1,),
    by2=(YB, NY - 1),
    by3=(YB,),
    s1=(NZ - 1,),
)
LOCAL = dict(fetch=(2 + FETCH,), out=(XS + YB,))


def main_kernel(g_ref, m_ref, r_ref, right_ref, ortho_ref, inv_ref, *scratch):
    names = [*BUFFERS, *LOCAL, *(n + e for n in REMOTE for e in ("_send", "_recv"))]
    ref = dict(zip(names, scratch, strict=True))
    gbuf, mbuf, rfac, bb, pbuf, pin, lbuf, lpin, lt = (ref[n] for n in list(BUFFERS)[:9])
    gp, gxin, gxs, gyin, gfull, ws = (ref[n] for n in list(BUFFERS)[9:15])
    mx, my, x1in, xs, y2in, y1in, ys, x2in, fx, fy, rv, sq = (ref[n] for n in list(BUFFERS)[15:])
    x, y, c, z = (lax.axis_index(a) for a in (*DP, "tensor"))
    pair = {"dp_2": 1 - c}
    pending = []

    def at_x(off):
        return lax.rem(x + off, NX)

    def at_y(off):
        return lax.rem(y + off, NY)

    def at_z(off):
        return lax.rem(z + off, NZ)

    def send(name, index, src, dst, where):
        copy = pltpu.make_async_remote_copy(
            src_ref=src,
            dst_ref=dst,
            send_sem=ref[name + "_send"].at[index],
            recv_sem=ref[name + "_recv"].at[index],
            device_id=where,
            device_id_type=MESH,
        )
        copy.start()
        pending.append(copy)
        return copy

    def arrive(copies):
        for copy in copies:
            copy.wait_recv()

    barrier = pltpu.get_barrier_semaphore()
    greet = [{"tensor": at_z(o)} for o in offsets(NZ)]
    greet += [{"dp_1": at_y(o)} for o in offsets(NY)]
    greet += [{"dp_0": at_x(o)} for o in offsets(NX)]
    greet += [pair]
    for where in greet:
        pl.semaphore_signal(barrier, inc=1, device_id=where, device_id_type=MESH)

    depth = LOCAL_COLS // FETCH
    fetches = [(g_ref, gbuf), (m_ref, mbuf)]
    fetches += [(r_ref.at[pl.ds(depth * i, depth)], rfac.at[pl.ds(depth * i, depth)]) for i in range(FETCH)]
    fetches = [pltpu.make_async_copy(src, dst, ref["fetch"].at[i]) for i, (src, dst) in enumerate(fetches)]
    for copy in fetches:
        copy.start()

    fetches[0].wait()
    fetches[1].wait()
    bb[0:LOCAL_ROWS, :] = gbuf[...] + mbuf[...]
    part = None
    for i in range(FETCH):
        fetches[2 + i].wait()
        more = dot(bb[0:LOCAL_ROWS, depth * i : depth * (i + 1)], rfac[depth * i : depth * (i + 1), :])
        part = more if part is None else part + more
    for i in range(NZ):
        pbuf[i] = part[8 * i : 8 * i + 8, :] if i < LEFT_CHUNKS else jnp.zeros((8, RANK), F32)
    pl.semaphore_wait(barrier, len(greet))

    copies = [(o, send("a1", o - 1, pbuf.at[at_z(o)], pin.at[o - 1], {"tensor": at_z(o)})) for o in offsets(NZ)]
    swap_b = send("swap", 0, bb.at[pl.ds(0, LOCAL_ROWS)], bb.at[pl.ds(LOCAL_ROWS, LOCAL_ROWS)], pair)
    total = pbuf[z]
    for o, copy in sorted(copies, key=lambda oc: oc[0]):
        copy.wait_recv()
        total = total + pin[o - 1]
    lbuf[z] = total
    copies = [send("a2", o - 1, lbuf.at[z], lbuf.at[z], {"tensor": at_z(o)}) for o in offsets(NZ)]
    arrive(copies)

    swap_left = send("swap", 1, lbuf.at[pl.ds(0, LEFT_CHUNKS)], lpin, pair)
    swap_left.wait_recv()
    swap_b.wait_recv()
    chip_left = jnp.concatenate([lbuf[i] for i in range(LEFT_CHUNKS)] + [lpin[i] for i in range(LEFT_CHUNKS)], axis=0)
    lt[...] = chip_left.T
    half = lt[pl.ds(pl.multiple_of(128 * c, 128), 128), :]
    gram = dot(half, chip_left)
    for i in range(NX):
        for j in range(NY):
            r0 = 8 * ((i // 2) * NY + j)
            gp[i, j] = gram[r0 : r0 + 8, 128 * (i % 2) : 128 * (i % 2) + 128]
    g1 = {o: send("g1", o - 1, gp.at[at_x(o)], gxin.at[o - 1], {"dp_0": at_x(o)}) for o in offsets(NX)}

    def product(t):
        d = dot(half, bb[:, 256 * t : 256 * t + 256])
        return d[:, 0:128].T, d[:, 128:256].T

    def product_x(s):
        for i in range(2):
            first, second = product(2 * s + i)
            mx[s, 2 * i] = first.reshape(NY, 16, 128)
            mx[s, 2 * i + 1] = second.reshape(NY, 16, 128)
        return {o: send("x1", (s, o - 1), mx.at[s, at_x(o)], x1in.at[s, o - 1], {"dp_0": at_x(o)}) for o in offsets(NX)}

    def product_y(b):
        first, second = product(2 * XS + b)
        my[b, 0:2] = first.reshape(2, NY, 8, 128)
        my[b, 2:4] = second.reshape(2, NY, 8, 128)

    def send_y1(b):
        return {o: send("y1", (b, o - 1), my.at[b, :, at_y(o)], y1in.at[b, o - 1], {"dp_1": at_y(o)}) for o in offsets(NY)}

    y1, x1, y2 = [None] * YB, [None] * XS, [None] * XS
    product_y(0)
    y1[0] = send_y1(0)
    x1[0] = product_x(0)
    product_y(1)
    x1[1] = product_x(1)
    product_y(2)
    x1[2] = product_x(2)

    def sum_x1(s):
        arrive(x1[s].values())
        for i in range(NY):
            acc = mx[s, x, i]
            for o in range(1, NX):
                acc = acc + x1in[s, o - 1, i]
            xs[s, i] = acc
        y2[s] = {o: send("y2", (s, o - 1), xs.at[s, at_y(o)], y2in.at[s, o - 1], {"dp_1": at_y(o)}) for o in offsets(NY)}

    def sum_y1(b):
        arrive(y1[b].values())
        for i in range(NX):
            acc = my[b, i, y]
            for o in range(1, NY):
                acc = acc + y1in[b, o - 1, i]
            ys[i, b] = acc

    arrive(g1.values())
    for j in range(NY):
        acc = gp[x, j]
        for o in range(1, NX):
            acc = acc + gxin[o - 1, j]
        gxs[j] = acc
    g2 = {o: send("g2", o - 1, gxs.at[at_y(o)], gyin.at[o - 1], {"dp_1": at_y(o)}) for o in offsets(NY)}
    y1[1] = send_y1(1)
    sum_x1(0)
    arrive(g2.values())
    acc = gxs[y]
    for o in range(1, NY):
        acc = acc + gyin[o - 1]
    gfull[c, x, y] = acc
    g3 = [send("g3", o - 1, gfull.at[c, x, y], gfull.at[c, x, y], {"dp_1": at_y(o)}) for o in offsets(NY)]
    y1[2] = send_y1(2)
    sum_x1(1)
    sum_y1(0)
    sum_x1(2)
    sum_y1(1)
    arrive(g3)
    g4 = [send("g4", o - 1, gfull.at[c, x], gfull.at[c, x], {"dp_0": at_x(o)}) for o in offsets(NX)]
    sum_y1(2)
    x2 = {o: send("x2", o - 1, ys.at[at_x(o)], x2in.at[o - 1], {"dp_0": at_x(o)}) for o in offsets(NX)}

    def back_x1(s):
        arrive(y2[s].values())
        acc = xs[s, y]
        for o in range(1, NY):
            acc = acc + y2in[s, o - 1]
        fx[c, s, x, y] = acc
        return [send("bx1", (s, o - 1), fx.at[c, s, x, y], fx.at[c, s, x, y], {"dp_1": at_y(o)}) for o in offsets(NY)]

    def back_x2(s):
        arrive(bx1[s])
        return [send("bx2", (s, o - 1), fx.at[c, s, x], fx.at[c, s, x], {"dp_0": at_x(o)}) for o in offsets(NX)]

    def back_x3(s):
        arrive(bx2[s])
        return send("bx3", s, fx.at[c, s], fx.at[c, s], pair)

    bx1, bx2, bx3, by2, by3 = [None] * XS, [None] * XS, [None] * XS, [None] * YB, [None] * YB
    bx1[0] = back_x1(0)
    arrive(g4)
    g5 = send("g5", 0, gfull.at[c], gfull.at[c], pair)
    bx1[1] = back_x1(1)
    bx1[2] = back_x1(2)
    arrive(x2.values())
    acc = ys[x]
    for o in range(1, NX):
        acc = acc + x2in[o - 1]
    fy[c, :, x, y] = acc
    by1 = [send("by1", o - 1, fy.at[c, :, x, y], fy.at[c, :, x, y], {"dp_0": at_x(o)}) for o in offsets(NX)]

    g5.wait_recv()
    for h in range(NC):
        for i in range(NX):
            for j in range(NY):
                r0 = 128 * h + 8 * ((i // 2) * NY + j)
                ws[r0 : r0 + 8, 128 * (i % 2) : 128 * (i % 2) + 128] = gfull[h, i, j]
    ri = lax.broadcasted_iota(jnp.int32, (RANK, RANK), 0)
    ci = lax.broadcasted_iota(jnp.int32, (RANK, RANK), 1)
    ws[:, RANK:] = jnp.where(ri == ci, 1.0, 0.0)

    factor_panel(ws, 0)
    arrive(by1)
    for b in range(YB):
        by2[b] = [
            send("by2", (b, o - 1), fy.at[c, b, :, y], fy.at[c, b, :, y], {"dp_1": at_y(o)}) for o in offsets(NY)
        ]
    factor_panel(ws, 1)
    bx2[0] = back_x2(0)
    factor_panel(ws, 2)
    bx2[1] = back_x2(1)
    factor_panel(ws, 3)
    bx2[2] = back_x2(2)
    inverse = ws[:, RANK:]
    ortho_ref[...] = dot(chip_left[0:LOCAL_ROWS, :], inverse, ((1,), (1,)))

    outs = []

    def right(parts, r0, n):
        d = dot(jnp.concatenate(parts, axis=1), ws[:, RANK:], ((1,), (1,)))
        rv[r0 : r0 + n, :] = d
        copy = pltpu.make_async_copy(rv.at[pl.ds(r0, n)], right_ref.at[pl.ds(r0, n)], ref["out"].at[len(outs)])
        copy.start()
        outs.append(copy)
        return jnp.sum(d * d, axis=0, keepdims=True)

    def right_x(s):
        bx3[s].wait_recv()
        return right([fx[h, s].reshape(512, 128) for h in range(NC)], 512 * s, 512)

    def right_y(b):
        by3[b].wait_recv()
        return right([fy[h, b].reshape(256, 128) for h in range(NC)], Y0 + 256 * b, 256)

    def back_y3(b):
        arrive(by2[b])
        return send("by3", b, fy.at[c, b], fy.at[c, b], pair)

    bx3[0] = back_x3(0)
    by3[0] = back_y3(0)
    squares = right_x(0)
    bx3[1] = back_x3(1)
    by3[1] = back_y3(1)
    squares = squares + right_y(0)
    squares = squares + right_x(1)
    squares = squares + right_y(1)
    bx3[2] = back_x3(2)
    by3[2] = back_y3(2)
    squares = squares + right_x(2)
    squares = squares + right_y(2)

    sq[z] = squares
    copies = [send("s1", o - 1, sq.at[z], sq.at[z], {"tensor": at_z(o)}) for o in offsets(NZ)]
    arrive(copies)
    total = sq[0]
    for i in range(1, NZ):
        total = total + sq[i]
    inv_ref[...] = 1.0 / jnp.sqrt(total / COLS + 1e-06)

    for copy in pending:
        copy.wait_send()
    for copy in outs:
        copy.wait()


def two_parts(a):
    big = a.astype(BF16)
    return big, (a - big.astype(F32)).astype(BF16)


def final_kernel(g_ref, m_ref, r_ref, ortho_ref, inv_ref, up_ref, nm_ref, nr_ref):
    ortho = ortho_ref[...]
    inv = inv_ref[...]
    r = r_ref[...]
    rows = jnp.concatenate([ortho * (inv * ((ROWS / RANK) ** 0.5)), ortho * 0.05], axis=0)
    rows_big, rows_small = two_parts(rows)
    r_big, r_small = two_parts(r)
    dims = (((1,), (1,)), ((), ()))
    both = lax.dot_general(rows_big, r_big, dims, preferred_element_type=F32)
    both = both + lax.dot_general(rows_big, r_small, dims, preferred_element_type=F32)
    both = both + lax.dot_general(rows_small, r_big, dims, preferred_element_type=F32)
    up_ref[...] = both[0:LOCAL_ROWS, :]
    nm_ref[...] = (g_ref[...] + m_ref[...]) - both[LOCAL_ROWS:, :]
    nr_ref[...] = r * inv


def on_device(gradient, momentum, right_factor):
    vmem = pl.BlockSpec(memory_space=pltpu.VMEM)
    hbm = pl.BlockSpec(memory_space=pl.ANY)
    dma = pltpu.SemaphoreType.DMA
    right, ortho, inv = pl.pallas_call(
        main_kernel,
        name="sums",
        out_shape=(
            jax.ShapeDtypeStruct((LOCAL_COLS, RANK), F32),
            jax.ShapeDtypeStruct((LOCAL_ROWS, RANK), F32),
            jax.ShapeDtypeStruct((1, RANK), F32),
        ),
        in_specs=[hbm] * 3,
        out_specs=[hbm, vmem, vmem],
        scratch_shapes=[pltpu.VMEM(shape, F32) for shape in BUFFERS.values()]
        + [dma(shape) for shape in LOCAL.values()]
        + [dma(shape) for shape in REMOTE.values() for _ in range(2)],
        compiler_params=pltpu.CompilerParams(
            collective_id=0, has_side_effects=True, vmem_limit_bytes=62 * 2**20
        ),
    )(gradient, momentum, right_factor)
    steps = 3
    width = LOCAL_COLS // steps
    wide = pl.BlockSpec((LOCAL_ROWS, width), lambda i: (0, i))
    tall = pl.BlockSpec((width, RANK), lambda i: (i, 0))
    return tuple(
        pl.pallas_call(
            final_kernel,
            name="outputs",
            grid=(steps,),
            out_shape=(
                jax.ShapeDtypeStruct((LOCAL_ROWS, LOCAL_COLS), F32),
                jax.ShapeDtypeStruct((LOCAL_ROWS, LOCAL_COLS), F32),
                jax.ShapeDtypeStruct((LOCAL_COLS, RANK), F32),
            ),
            in_specs=[
                wide,
                wide,
                tall,
                pl.BlockSpec((LOCAL_ROWS, RANK), lambda i: (0, 0)),
                pl.BlockSpec((1, RANK), lambda i: (0, 0)),
            ],
            out_specs=[wide, wide, tall],
        )(gradient, momentum, right, ortho, inv)
    )


def solution(mesh):
    finer = Mesh(mesh.devices.reshape(NX, NY, NC, mesh.shape["tensor"]), (*DP, "tensor"))
    return jax.shard_map(
        on_device,
        mesh=finer,
        in_specs=(P(DP, "tensor"), P(DP, "tensor"), P("tensor", None)),
        out_specs=(P(DP, "tensor"), P(DP, "tensor"), P("tensor", None)),
        check_vma=False,
    )
```

time: 554 us -> 89.8 us (0.16)
  blocking collectives: 243 us -> 0 us
  waiting for transfers between devices: 197 us -> 0 us
  Pallas kernels: 0 us -> 89 us
  other arithmetic: 64.2 us -> 0 us
  matrix products: 19.2 us -> 0 us
  between operations: 15.5 us -> 0.64 us
  local copies, waits for them, and re-layouts: 14.6 us -> 0 us
    psum x1 -> x0, waiting for transfers between devices: 197 us -> none  [on_device(): lax.psum(jnp.dot(left.T, left, precision=high, preferred_element_type=jnp...]
    all_to_all x3 -> x0, blocking collectives: 195 us -> none  [the longest x2 126 us: sent_to_all(): return lax.all_to_all(copies, axis, split_axis=0, concat_axis=0, tiled=True)]
    pallas_call x0 -> x2, Pallas kernels: none -> 89 us  [the longest x1 83 us: on_device(): pl.pallas_call(main_kernel, name='sums', out_shape=(jax.ShapeDtypeStruct(...]
    another operation x9 -> x0, other arithmetic: 58.4 us -> none  [the longest x6 36.3 us: on_device(): chol = jnp.linalg.cholesky(gram)]
    psum x4 -> x0, blocking collectives: 47.8 us -> none  [over_axes(): value = lax.psum(value, axis)]
    dot_general x5 -> x0, matrix products: 14.1 us -> none  [the longest x1 4.97 us: on_device(): jnp.dot(ortho, right.T, precision=high, preferred_element_type=jnp.float32)]
    reshape x2 -> x0, local copies, waits for them, and re-layouts: 6.71 us -> none  [the longest x1 3.39 us: laid_out(): return jnp.moveaxis(blocks, 0, dim).reshape(lengths)]
  transfers between devices with their start and end apart: 1 -> 0, of which waited for: 1 -> 0; matrix products, arithmetic and copies ran while one was open for 0% -> 0% of each run, Pallas kernels for 0% -> 0%
where the time goes in v2:
time: 89.8 us; the launch traced here: 89.6 us
  Pallas kernels  89 us (99%)
    pallas_call x1, Pallas kernels, on_device(): pl.pallas_call(main_kernel, name='sums', out_shape=(jax.ShapeDtypeStruct(...  83 us
    pallas_call x1, Pallas kernels, on_device(): pl.pallas_call(final_kernel, name='outputs', grid=(steps,), out_shape=(ja...  5.94 us

profile of v2, /device:TPU:1, one launch (start us, length us, event | category | flops | bytes accessed | tf_op | source)
XLA Modules:
  0.0 89.6 jit_solution(10305141970965600332)
XLA Ops:
  0.6 83.0 %sums.1 = (f32[2304,256]{1,0:T(8,128)}, f32[80,256]{1,0:T(8,128)}, f32[1,256]{1,0:T(1,128)}) custom-call(f32[80,2304]{1,0:T(8,128)} %g_ref.3, f32[80,2304]{1,0:T(8,128)} %m_ref.3, f32[2304,256]{1,0:T(8,128)} %r_ref.1), custom_call_target="tpu_custom_call" | custom-call | tf_op jit(solution)/shard_map/sums/pallas_call | solution.py:410
  83.7 5.9 %outputs.1 = (f32[80,2304]{1,0:T(8,128)}, f32[80,2304]{1,0:T(8,128)}, f32[2304,256]{1,0:T(8,128)}) custom-call(f32[80,2304]{1,0:T(8,128)} %g_ref.3, f32[80,2304]{1,0:T(8,128)} %m_ref.3, f32[2304,256]{1,0:T(8,128)} %get-tuple-element.6.r_ref, f32[80,256]{1,0:T(8,128)} %get-tuple-element.7.ortho_ref, f32[1,256]{1,0:T(1,128)} %get-tuple-element.8.inv_ref), custom_call_target="tpu_custom_call" | custom-call | tf_op jit(solution)/shard_map/outputs/pallas_call | solution.py:432

commit v3 on v2

--- a/solution.py
+++ b/solution.py
@@ -23,6 +23,7 @@
 Y0 = 512 * XS
 FETCH = 3
 PANEL = 64
+SLAB = 16
 
 
 def dot(a, b, dims=((1,), (0,))):
@@ -30,20 +31,20 @@
 
 
 def eliminate_slab(ws, p, s):
-    r0 = PANEL * p + 8 * s
+    r0 = PANEL * p + SLAB * s
     end = PANEL * (p + 1)
     n = end - r0
     lo = (r0 // 128) * 128
     hi = RANK + (r0 // 128 + 1) * 128
-    cols = [jnp.broadcast_to(ws[r0:end, r0 + j : r0 + j + 1], (n, 128)) for j in range(8)]
+    cols = [jnp.broadcast_to(ws[r0:end, r0 + j : r0 + j + 1], (n, 128)) for j in range(SLAB)]
     w = ws[r0:end, lo:hi]
     sub = lax.broadcasted_iota(jnp.int32, (n, 128), 0)
     wide_sub = lax.broadcasted_iota(jnp.int32, w.shape, 0)
     reps = (hi - lo) // 128
-    for j in range(8):
+    for j in range(SLAB):
         rs = lax.rsqrt(cols[j][j : j + 1, :])
         l = cols[j] * rs
-        for m in range(j + 1, 8):
+        for m in range(j + 1, SLAB):
             cols[m] = cols[m] - l * l[m : m + 1, :]
         lm = jnp.concatenate([jnp.where(sub > j, l, 0.0)] * reps, axis=1)
         u = w[j : j + 1, :] * jnp.concatenate([rs] * reps, axis=1)
@@ -59,9 +60,13 @@
     ws[b:RANK, lo:hi] = ws[b:RANK, lo:hi] - full[b - lo :, :]
 
 
+def factor_slabs(ws, p, first, last):
+    for s in range(first, last):
+        eliminate_slab(ws, p, s)
+
+
 def factor_panel(ws, p):
-    for s in range(PANEL // 8):
-        eliminate_slab(ws, p, s)
+    factor_slabs(ws, p, 0, PANEL // SLAB)
     if PANEL * (p + 1) < RANK:
         update_below(ws, p)
 
@@ -98,6 +103,11 @@
     fy=(NC, YB, NX, NY, 8, 128),
     rv=(LOCAL_COLS, RANK),
     sq=(NZ, 1, RANK),
+    ex=(NC, XS, NY, 16, 128),
+    ey=(NC, YB, NX, 8, 128),
+    vx=(NX, 1, RANK),
+    vy=(NY, 1, RANK),
+    tinv=(RANK, RANK),
 )
 REMOTE = dict(
     swap=(2,),
@@ -119,8 +129,12 @@
     by2=(YB, NY - 1),
     by3=(YB,),
     s1=(NZ - 1,),
+    px=(XS,),
+    py=(1,),
+    v1=(NX - 1,),
+    v2=(NY - 1,),
 )
-LOCAL = dict(fetch=(2 + FETCH,), out=(XS + YB,))
+LOCAL = dict(fetch=(3 * FETCH,), out=(XS + YB,))
 
 
 def main_kernel(g_ref, m_ref, r_ref, right_ref, ortho_ref, inv_ref, *scratch):
@@ -128,7 +142,7 @@
     ref = dict(zip(names, scratch, strict=True))
     gbuf, mbuf, rfac, bb, pbuf, pin, lbuf, lpin, lt = (ref[n] for n in list(BUFFERS)[:9])
     gp, gxin, gxs, gyin, gfull, ws = (ref[n] for n in list(BUFFERS)[9:15])
-    mx, my, x1in, xs, y2in, y1in, ys, x2in, fx, fy, rv, sq = (ref[n] for n in list(BUFFERS)[15:])
+    mx, my, x1in, xs, y2in, y1in, ys, x2in, fx, fy, rv, sq, ex, ey, vx, vy, tinv = (ref[n] for n in list(BUFFERS)[15:])
     x, y, c, z = (lax.axis_index(a) for a in (*DP, "tensor"))
     pair = {"dp_2": 1 - c}
     pending = []
@@ -168,19 +182,27 @@
         pl.semaphore_signal(barrier, inc=1, device_id=where, device_id_type=MESH)
 
     depth = LOCAL_COLS // FETCH
-    fetches = [(g_ref, gbuf), (m_ref, mbuf)]
-    fetches += [(r_ref.at[pl.ds(depth * i, depth)], rfac.at[pl.ds(depth * i, depth)]) for i in range(FETCH)]
-    fetches = [pltpu.make_async_copy(src, dst, ref["fetch"].at[i]) for i, (src, dst) in enumerate(fetches)]
+    fetches = []
+    for i in range(FETCH):
+        cols = pl.ds(depth * i, depth)
+        for j, (src, dst) in enumerate(
+            [
+                (g_ref.at[:, cols], gbuf.at[:, cols]),
+                (m_ref.at[:, cols], mbuf.at[:, cols]),
+                (r_ref.at[cols], rfac.at[cols]),
+            ]
+        ):
+            fetches.append(pltpu.make_async_copy(src, dst, ref["fetch"].at[3 * i + j]))
     for copy in fetches:
         copy.start()
 
-    fetches[0].wait()
-    fetches[1].wait()
-    bb[0:LOCAL_ROWS, :] = gbuf[...] + mbuf[...]
     part = None
     for i in range(FETCH):
-        fetches[2 + i].wait()
-        more = dot(bb[0:LOCAL_ROWS, depth * i : depth * (i + 1)], rfac[depth * i : depth * (i + 1), :])
+        for j in range(3):
+            fetches[3 * i + j].wait()
+        cols = slice(depth * i, depth * (i + 1))
+        bb[0:LOCAL_ROWS, cols] = gbuf[:, cols] + mbuf[:, cols]
+        more = dot(bb[0:LOCAL_ROWS, cols], rfac[cols, :])
         part = more if part is None else part + more
     for i in range(NZ):
         pbuf[i] = part[8 * i : 8 * i + 8, :] if i < LEFT_CHUNKS else jnp.zeros((8, RANK), F32)
@@ -289,13 +311,17 @@
 
     def back_x2(s):
         arrive(bx1[s])
+        px[s] = send("px", s, fx.at[c, s, x], ex.at[c, s], pair)
+        ex[c, s] = fx[c, s, x]
+
+    def send_x2(s):
         return [send("bx2", (s, o - 1), fx.at[c, s, x], fx.at[c, s, x], {"dp_0": at_x(o)}) for o in offsets(NX)]
 
     def back_x3(s):
         arrive(bx2[s])
         return send("bx3", s, fx.at[c, s], fx.at[c, s], pair)
 
-    bx1, bx2, bx3, by2, by3 = [None] * XS, [None] * XS, [None] * XS, [None] * YB, [None] * YB
+    px, bx1, bx2, bx3, by2, by3 = [None] * XS, [None] * XS, [None] * XS, [None] * XS, [None] * YB, [None] * YB
     bx1[0] = back_x1(0)
     arrive(g4)
     g5 = send("g5", 0, gfull.at[c], gfull.at[c], pair)
@@ -319,37 +345,57 @@
     ws[:, RANK:] = jnp.where(ri == ci, 1.0, 0.0)
 
     factor_panel(ws, 0)
+    back_x2(0)
+    bx2[0] = send_x2(0)
+    half_panel = PANEL // SLAB // 2
+    factor_slabs(ws, 1, 0, half_panel)
     arrive(by1)
-    for b in range(YB):
-        by2[b] = [
-            send("by2", (b, o - 1), fy.at[c, b, :, y], fy.at[c, b, :, y], {"dp_1": at_y(o)}) for o in offsets(NY)
-        ]
-    factor_panel(ws, 1)
-    bx2[0] = back_x2(0)
+
+    def send_y2(b):
+        return [send("by2", (b, o - 1), fy.at[c, b, :, y], fy.at[c, b, :, y], {"dp_1": at_y(o)}) for o in offsets(NY)]
+
+    by2[0] = send_y2(0)
+    by2[1] = send_y2(1)
+    py = send("py", 0, fy.at[c, :, :, y], ey.at[c], pair)
+    ey[c] = fy[c, :, :, y]
+    factor_slabs(ws, 1, half_panel, 2 * half_panel)
+    update_below(ws, 1)
+    back_x2(1)
+    bx2[1] = send_x2(1)
     factor_panel(ws, 2)
-    bx2[1] = back_x2(1)
+    back_x2(2)
     factor_panel(ws, 3)
-    bx2[2] = back_x2(2)
-    inverse = ws[:, RANK:]
-    ortho_ref[...] = dot(chip_left[0:LOCAL_ROWS, :], inverse, ((1,), (1,)))
+    tinv[...] = ws[:, RANK:].T
+
+    def square_sum(parts):
+        d = dot(jnp.concatenate(parts, axis=1), tinv[...])
+        return jnp.sum(d * d, axis=0, keepdims=True)
+
+    arrive(px)
+    py.wait_recv()
+    vx[x] = square_sum([ex[h].reshape(128 * XS, 128) for h in range(NC)])
+    v1 = [send("v1", o - 1, vx.at[x], vx.at[x], {"dp_0": at_x(o)}) for o in offsets(NX)]
+    bx2[2] = send_x2(2)
+    vy[y] = square_sum([ey[h].reshape(8 * NX * YB, 128) for h in range(NC)])
+    v2 = [send("v2", o - 1, vy.at[y], vy.at[y], {"dp_1": at_y(o)}) for o in offsets(NY)]
+    by2[2] = send_y2(2)
+    ortho_ref[...] = dot(chip_left[0:LOCAL_ROWS, :], tinv[...])
 
     outs = []
 
     def right(parts, r0, n):
-        d = dot(jnp.concatenate(parts, axis=1), ws[:, RANK:], ((1,), (1,)))
-        rv[r0 : r0 + n, :] = d
+        rv[r0 : r0 + n, :] = dot(jnp.concatenate(parts, axis=1), tinv[...])
         copy = pltpu.make_async_copy(rv.at[pl.ds(r0, n)], right_ref.at[pl.ds(r0, n)], ref["out"].at[len(outs)])
         copy.start()
         outs.append(copy)
-        return jnp.sum(d * d, axis=0, keepdims=True)
 
     def right_x(s):
         bx3[s].wait_recv()
-        return right([fx[h, s].reshape(512, 128) for h in range(NC)], 512 * s, 512)
+        right([fx[h, s].reshape(512, 128) for h in range(NC)], 512 * s, 512)
 
     def right_y(b):
         by3[b].wait_recv()
-        return right([fy[h, b].reshape(256, 128) for h in range(NC)], Y0 + 256 * b, 256)
+        right([fy[h, b].reshape(256, 128) for h in range(NC)], Y0 + 256 * b, 256)
 
     def back_y3(b):
         arrive(by2[b])
@@ -357,20 +403,27 @@
 
     bx3[0] = back_x3(0)
     by3[0] = back_y3(0)
-    squares = right_x(0)
+    right_x(0)
     bx3[1] = back_x3(1)
+    right_y(0)
+    right_x(1)
     by3[1] = back_y3(1)
-    squares = squares + right_y(0)
-    squares = squares + right_x(1)
-    squares = squares + right_y(1)
+    arrive(v1)
+    arrive(v2)
+    total = vx[0]
+    for i in range(1, NX):
+        total = total + vx[i]
+    for i in range(NY):
+        total = total + vy[i]
+    sq[z] = total
+    s1 = [send("s1", o - 1, sq.at[z], sq.at[z], {"tensor": at_z(o)}) for o in offsets(NZ)]
     bx3[2] = back_x3(2)
+    right_y(1)
     by3[2] = back_y3(2)
-    squares = squares + right_x(2)
-    squares = squares + right_y(2)
-
-    sq[z] = squares
-    copies = [send("s1", o - 1, sq.at[z], sq.at[z], {"tensor": at_z(o)}) for o in offsets(NZ)]
-    arrive(copies)
+    right_x(2)
+    right_y(2)
+
+    arrive(s1)
     total = sq[0]
     for i in range(1, NZ):
         total = total + sq[i]
@@ -424,7 +477,7 @@
             collective_id=0, has_side_effects=True, vmem_limit_bytes=62 * 2**20
         ),
     )(gradient, momentum, right_factor)
-    steps = 3
+    steps = 2
     width = LOCAL_COLS // steps
     wide = pl.BlockSpec((LOCAL_ROWS, width), lambda i: (0, i))
     tall = pl.BlockSpec((width, RANK), lambda i: (i, 0))

time: 89.8 us -> 81.1 us (0.903)
  Pallas kernels: 89 us -> 80.3 us
    pallas_call x1, Pallas kernels: 83 us -> 76.1 us  [on_device(): pl.pallas_call(main_kernel, name='sums', out_shape=(jax.ShapeDtypeStruct(...]
    pallas_call x1, Pallas kernels: 5.94 us -> 4.26 us  [on_device(): pl.pallas_call(final_kernel, name='outputs', grid=(steps,), out_shape=(ja...]
where the time goes in v3:
time: 81.1 us; the launch traced here: 81 us
  Pallas kernels  80.3 us (99%)
    pallas_call x1, Pallas kernels, on_device(): pl.pallas_call(main_kernel, name='sums', out_shape=(jax.ShapeDtypeStruct(...  76.1 us
    pallas_call x1, Pallas kernels, on_device(): pl.pallas_call(final_kernel, name='outputs', grid=(steps,), out_shape=(ja...  4.26 us

profile of v3, /device:TPU:1, one launch (start us, length us, event | category | flops | bytes accessed | tf_op | source)
XLA Modules:
  0.0 81.0 jit_solution(4875833679409352924)
XLA Ops:
  0.6 76.1 %sums.1 = (f32[2304,256]{1,0:T(8,128)}, f32[80,256]{1,0:T(8,128)}, f32[1,256]{1,0:T(1,128)}) custom-call(f32[80,2304]{1,0:T(8,128)} %g_ref.3, f32[80,2304]{1,0:T(8,128)} %m_ref.3, f32[2304,256]{1,0:T(8,128)} %r_ref.1), custom_call_target="tpu_custom_call" | custom-call | tf_op jit(solution)/shard_map/sums/pallas_call | solution.py:463
  76.7 4.3 %outputs.1 = (f32[80,2304]{1,0:T(8,128)}, f32[80,2304]{1,0:T(8,128)}, f32[2304,256]{1,0:T(8,128)}) custom-call(f32[80,2304]{1,0:T(8,128)} %g_ref.3, f32[80,2304]{1,0:T(8,128)} %m_ref.3, f32[2304,256]{1,0:T(8,128)} %get-tuple-element.6.r_ref, f32[80,256]{1,0:T(8,128)} %get-tuple-element.7.ortho_ref, f32[1,256]{1,0:T(1,128)} %get-tuple-element.8.inv_ref), custom_call_target="tpu_custom_call" | custom-call | tf_op jit(solution)/shard_map/outputs/pallas_call | solution.py:485

commit v4 on v3

--- a/solution.py
+++ b/solution.py
@@ -22,6 +22,7 @@
 XS, YB = 3, 3
 Y0 = 512 * XS
 FETCH = 3
+OUT_PARTS = 3
 PANEL = 64
 SLAB = 16
 
@@ -101,7 +102,6 @@
     x2in=(NX - 1, YB, 8, 128),
     fx=(NC, XS, NX, NY, 16, 128),
     fy=(NC, YB, NX, NY, 8, 128),
-    rv=(LOCAL_COLS, RANK),
     sq=(NZ, 1, RANK),
     ex=(NC, XS, NY, 16, 128),
     ey=(NC, YB, NX, 8, 128),
@@ -134,15 +134,15 @@
     v1=(NX - 1,),
     v2=(NY - 1,),
 )
-LOCAL = dict(fetch=(3 * FETCH,), out=(XS + YB,))
-
-
-def main_kernel(g_ref, m_ref, r_ref, right_ref, ortho_ref, inv_ref, *scratch):
+LOCAL = dict(fetch=(3 * FETCH,))
+
+
+def main_kernel(g_ref, m_ref, r_ref, right_ref, ortho_ref, inv_ref, b_ref, *scratch):
     names = [*BUFFERS, *LOCAL, *(n + e for n in REMOTE for e in ("_send", "_recv"))]
     ref = dict(zip(names, scratch, strict=True))
     gbuf, mbuf, rfac, bb, pbuf, pin, lbuf, lpin, lt = (ref[n] for n in list(BUFFERS)[:9])
     gp, gxin, gxs, gyin, gfull, ws = (ref[n] for n in list(BUFFERS)[9:15])
-    mx, my, x1in, xs, y2in, y1in, ys, x2in, fx, fy, rv, sq, ex, ey, vx, vy, tinv = (ref[n] for n in list(BUFFERS)[15:])
+    mx, my, x1in, xs, y2in, y1in, ys, x2in, fx, fy, sq, ex, ey, vx, vy, tinv = (ref[n] for n in list(BUFFERS)[15:])
     x, y, c, z = (lax.axis_index(a) for a in (*DP, "tensor"))
     pair = {"dp_2": 1 - c}
     pending = []
@@ -326,14 +326,6 @@
     arrive(g4)
     g5 = send("g5", 0, gfull.at[c], gfull.at[c], pair)
     bx1[1] = back_x1(1)
-    bx1[2] = back_x1(2)
-    arrive(x2.values())
-    acc = ys[x]
-    for o in range(1, NX):
-        acc = acc + x2in[o - 1]
-    fy[c, :, x, y] = acc
-    by1 = [send("by1", o - 1, fy.at[c, :, x, y], fy.at[c, :, x, y], {"dp_0": at_x(o)}) for o in offsets(NX)]
-
     g5.wait_recv()
     for h in range(NC):
         for i in range(NX):
@@ -344,11 +336,23 @@
     ci = lax.broadcasted_iota(jnp.int32, (RANK, RANK), 1)
     ws[:, RANK:] = jnp.where(ri == ci, 1.0, 0.0)
 
-    factor_panel(ws, 0)
+    half_panel = PANEL // SLAB // 2
+    factor_slabs(ws, 0, 0, 1)
+    bx1[2] = back_x1(2)
+    arrive(x2.values())
+    acc = ys[x]
+    for o in range(1, NX):
+        acc = acc + x2in[o - 1]
+    fy[c, :, x, y] = acc
+    by1 = [send("by1", o - 1, fy.at[c, :, x, y], fy.at[c, :, x, y], {"dp_0": at_x(o)}) for o in offsets(NX)]
+
+    factor_slabs(ws, 0, 1, 2 * half_panel)
+    update_below(ws, 0)
     back_x2(0)
     bx2[0] = send_x2(0)
-    half_panel = PANEL // SLAB // 2
     factor_slabs(ws, 1, 0, half_panel)
+    factor_slabs(ws, 1, half_panel, 2 * half_panel)
+    update_below(ws, 1)
     arrive(by1)
 
     def send_y2(b):
@@ -358,8 +362,6 @@
     by2[1] = send_y2(1)
     py = send("py", 0, fy.at[c, :, :, y], ey.at[c], pair)
     ey[c] = fy[c, :, :, y]
-    factor_slabs(ws, 1, half_panel, 2 * half_panel)
-    update_below(ws, 1)
     back_x2(1)
     bx2[1] = send_x2(1)
     factor_panel(ws, 2)
@@ -379,15 +381,11 @@
     vy[y] = square_sum([ey[h].reshape(8 * NX * YB, 128) for h in range(NC)])
     v2 = [send("v2", o - 1, vy.at[y], vy.at[y], {"dp_1": at_y(o)}) for o in offsets(NY)]
     by2[2] = send_y2(2)
+    b_ref[...] = bb[0:LOCAL_ROWS, :]
     ortho_ref[...] = dot(chip_left[0:LOCAL_ROWS, :], tinv[...])
 
-    outs = []
-
     def right(parts, r0, n):
-        rv[r0 : r0 + n, :] = dot(jnp.concatenate(parts, axis=1), tinv[...])
-        copy = pltpu.make_async_copy(rv.at[pl.ds(r0, n)], right_ref.at[pl.ds(r0, n)], ref["out"].at[len(outs)])
-        copy.start()
-        outs.append(copy)
+        right_ref[r0 : r0 + n, :] = dot(jnp.concatenate(parts, axis=1), tinv[...])
 
     def right_x(s):
         bx3[s].wait_recv()
@@ -406,8 +404,6 @@
     right_x(0)
     bx3[1] = back_x3(1)
     right_y(0)
-    right_x(1)
-    by3[1] = back_y3(1)
     arrive(v1)
     arrive(v2)
     total = vx[0]
@@ -417,6 +413,8 @@
         total = total + vy[i]
     sq[z] = total
     s1 = [send("s1", o - 1, sq.at[z], sq.at[z], {"tensor": at_z(o)}) for o in offsets(NZ)]
+    by3[1] = back_y3(1)
+    right_x(1)
     bx3[2] = back_x3(2)
     right_y(1)
     by3[2] = back_y3(2)
@@ -431,8 +429,6 @@
 
     for copy in pending:
         copy.wait_send()
-    for copy in outs:
-        copy.wait()
 
 
 def two_parts(a):
@@ -440,66 +436,72 @@
     return big, (a - big.astype(F32)).astype(BF16)
 
 
-def final_kernel(g_ref, m_ref, r_ref, ortho_ref, inv_ref, up_ref, nm_ref, nr_ref):
+def final_kernel(b_ref, r_ref, ortho_ref, inv_ref, up_ref, nm_ref, nr_ref, up, nm, nr, sems):
     ortho = ortho_ref[...]
     inv = inv_ref[...]
-    r = r_ref[...]
     rows = jnp.concatenate([ortho * (inv * ((ROWS / RANK) ** 0.5)), ortho * 0.05], axis=0)
     rows_big, rows_small = two_parts(rows)
-    r_big, r_small = two_parts(r)
     dims = (((1,), (1,)), ((), ()))
-    both = lax.dot_general(rows_big, r_big, dims, preferred_element_type=F32)
-    both = both + lax.dot_general(rows_big, r_small, dims, preferred_element_type=F32)
-    both = both + lax.dot_general(rows_small, r_big, dims, preferred_element_type=F32)
-    up_ref[...] = both[0:LOCAL_ROWS, :]
-    nm_ref[...] = (g_ref[...] + m_ref[...]) - both[LOCAL_ROWS:, :]
-    nr_ref[...] = r * inv
+    copies = []
+
+    def put(src, dst):
+        copy = pltpu.make_async_copy(src, dst, sems.at[len(copies)])
+        copy.start()
+        copies.append(copy)
+
+    width = LOCAL_COLS // OUT_PARTS
+    for i in range(OUT_PARTS):
+        span = slice(width * i, width * (i + 1))
+        here = pl.ds(width * i, width)
+        r = r_ref[span, :]
+        nr[span, :] = r * inv
+        put(nr.at[here], nr_ref.at[here])
+        r_big, r_small = two_parts(r)
+        both = lax.dot_general(rows_big, r_big, dims, preferred_element_type=F32)
+        both = both + lax.dot_general(rows_big, r_small, dims, preferred_element_type=F32)
+        both = both + lax.dot_general(rows_small, r_big, dims, preferred_element_type=F32)
+        up[:, span] = both[0:LOCAL_ROWS, :]
+        put(up.at[:, here], up_ref.at[:, here])
+        nm[:, span] = b_ref[:, span] - both[LOCAL_ROWS:, :]
+        put(nm.at[:, here], nm_ref.at[:, here])
+    for copy in copies:
+        copy.wait()
 
 
 def on_device(gradient, momentum, right_factor):
     vmem = pl.BlockSpec(memory_space=pltpu.VMEM)
-    hbm = pl.BlockSpec(memory_space=pl.ANY)
+    hbm = pl.BlockSpec(memory_space=pltpu.HBM)
     dma = pltpu.SemaphoreType.DMA
-    right, ortho, inv = pl.pallas_call(
+    shape = lambda *lengths: jax.ShapeDtypeStruct(lengths, F32)
+    right, ortho, inv, buffer = pl.pallas_call(
         main_kernel,
         name="sums",
         out_shape=(
-            jax.ShapeDtypeStruct((LOCAL_COLS, RANK), F32),
-            jax.ShapeDtypeStruct((LOCAL_ROWS, RANK), F32),
-            jax.ShapeDtypeStruct((1, RANK), F32),
+            pltpu.VMEM((LOCAL_COLS, RANK), F32),
+            pltpu.VMEM((LOCAL_ROWS, RANK), F32),
+            pltpu.VMEM((1, RANK), F32),
+            pltpu.VMEM((LOCAL_ROWS, LOCAL_COLS), F32),
         ),
         in_specs=[hbm] * 3,
-        out_specs=[hbm, vmem, vmem],
-        scratch_shapes=[pltpu.VMEM(shape, F32) for shape in BUFFERS.values()]
-        + [dma(shape) for shape in LOCAL.values()]
-        + [dma(shape) for shape in REMOTE.values() for _ in range(2)],
+        out_specs=[vmem] * 4,
+        scratch_shapes=[pltpu.VMEM(lengths, F32) for lengths in BUFFERS.values()]
+        + [dma(lengths) for lengths in LOCAL.values()]
+        + [dma(lengths) for lengths in REMOTE.values() for _ in range(2)],
         compiler_params=pltpu.CompilerParams(
-            collective_id=0, has_side_effects=True, vmem_limit_bytes=62 * 2**20
+            collective_id=0, has_side_effects=True, vmem_limit_bytes=59_000_000
         ),
     )(gradient, momentum, right_factor)
-    steps = 2
-    width = LOCAL_COLS // steps
-    wide = pl.BlockSpec((LOCAL_ROWS, width), lambda i: (0, i))
-    tall = pl.BlockSpec((width, RANK), lambda i: (i, 0))
+    outs = (shape(LOCAL_ROWS, LOCAL_COLS), shape(LOCAL_ROWS, LOCAL_COLS), shape(LOCAL_COLS, RANK))
     return tuple(
         pl.pallas_call(
             final_kernel,
             name="outputs",
-            grid=(steps,),
-            out_shape=(
-                jax.ShapeDtypeStruct((LOCAL_ROWS, LOCAL_COLS), F32),
-                jax.ShapeDtypeStruct((LOCAL_ROWS, LOCAL_COLS), F32),
-                jax.ShapeDtypeStruct((LOCAL_COLS, RANK), F32),
-            ),
-            in_specs=[
-                wide,
-                wide,
-                tall,
-                pl.BlockSpec((LOCAL_ROWS, RANK), lambda i: (0, 0)),
-                pl.BlockSpec((1, RANK), lambda i: (0, 0)),
-            ],
-            out_specs=[wide, wide, tall],
-        )(gradient, momentum, right, ortho, inv)
+            out_shape=outs,
+            in_specs=[vmem] * 4,
+            out_specs=[hbm] * 3,
+            scratch_shapes=[pltpu.VMEM(out.shape, F32) for out in outs] + [dma((3 * OUT_PARTS,))],
+            compiler_params=pltpu.CompilerParams(vmem_limit_bytes=24 * 2**20),
+        )(buffer, right, ortho, inv)
     )
 
 

time: 81.1 us -> 78.5 us (0.968)
  Pallas kernels: 80.3 us -> 77.6 us
    pallas_call x2, Pallas kernels: 80.3 us -> 77.6 us  [the longest x1 74.9 us: on_device(): pl.pallas_call(main_kernel, name='sums', out_shape=(pltpu.VMEM((LOCAL_COL...]
where the time goes in v4:
time: 78.5 us; the launch traced here: 78.4 us
  Pallas kernels  77.6 us (99%)
  between operations  0.8 us (1%)
    pallas_call x1, Pallas kernels, on_device(): pl.pallas_call(main_kernel, name='sums', out_shape=(pltpu.VMEM((LOCAL_COL...  74.9 us
    pallas_call x1, Pallas kernels, on_device(): pl.pallas_call(final_kernel, name='outputs', out_shape=outs, in_specs=[vm...  2.64 us

profile of v4, /device:TPU:1, one launch (start us, length us, event | category | flops | bytes accessed | tf_op | source)
XLA Modules:
  0.0 78.4 jit_solution(5210542398848286241)
XLA Ops:
  0.6 74.9 %sums.1 = (f32[2304,256]{1,0:T(8,128)S(1)}, f32[80,256]{1,0:T(8,128)S(1)}, f32[1,256]{1,0:T(1,128)S(1)}, f32[80,2304]{1,0:T(8,128)S(1)}) custom-call(f32[80,2304]{1,0:T(8,128)} %g_ref.1, f32[80,2304]{1,0:T(8,128)} %m_ref.1, f32[2304,256]{1,0:T(8,128)} %r_ref.1), custom_call_target="tpu_custom_call" | custom-call | tf_op jit(solution)/shard_map/sums/pallas_call | solution.py:476
  75.6 2.6 %outputs.1 = (f32[80,2304]{1,0:T(8,128)}, f32[80,2304]{1,0:T(8,128)}, f32[2304,256]{1,0:T(8,128)}) custom-call(f32[80,2304]{1,0:T(8,128)S(1)} %get-tuple-element.7.b_ref, f32[2304,256]{1,0:T(8,128)S(1)} %get-tuple-element.8.r_ref, f32[80,256]{1,0:T(8,128)S(1)} %get-tuple-element.9.ortho_ref, f32[1,256]{1,0:T(1,128)S(1)} %get-tuple-element.10.inv_ref), custom_call_target="tpu_custom_call" | custom-call | tf_op jit(solution)/shard_map/outputs/pallas_call | solution.py:496

commit v5 on v4

--- a/solution.py
+++ b/solution.py
@@ -173,14 +173,6 @@
         for copy in copies:
             copy.wait_recv()
 
-    barrier = pltpu.get_barrier_semaphore()
-    greet = [{"tensor": at_z(o)} for o in offsets(NZ)]
-    greet += [{"dp_1": at_y(o)} for o in offsets(NY)]
-    greet += [{"dp_0": at_x(o)} for o in offsets(NX)]
-    greet += [pair]
-    for where in greet:
-        pl.semaphore_signal(barrier, inc=1, device_id=where, device_id_type=MESH)
-
     depth = LOCAL_COLS // FETCH
     fetches = []
     for i in range(FETCH):
@@ -195,6 +187,14 @@
             fetches.append(pltpu.make_async_copy(src, dst, ref["fetch"].at[3 * i + j]))
     for copy in fetches:
         copy.start()
+
+    barrier = pltpu.get_barrier_semaphore()
+    greet = [{"tensor": at_z(o)} for o in offsets(NZ)]
+    greet += [{"dp_1": at_y(o)} for o in offsets(NY)]
+    greet += [{"dp_0": at_x(o)} for o in offsets(NX)]
+    greet += [pair]
+    for where in greet:
+        pl.semaphore_signal(barrier, inc=1, device_id=where, device_id_type=MESH)
 
     part = None
     for i in range(FETCH):

time: 78.5 us -> 78 us (level)
  no operation moved by 1% of the time
where the time goes in v5:
time: 78 us; the launch traced here: 77.9 us
  Pallas kernels  77.1 us (99%)
  between operations  0.8 us (1%)
    pallas_call x1, Pallas kernels, on_device(): pl.pallas_call(main_kernel, name='sums', out_shape=(pltpu.VMEM((LOCAL_COL...  74.5 us
    pallas_call x1, Pallas kernels, on_device(): pl.pallas_call(final_kernel, name='outputs', out_shape=outs, in_specs=[vm...  2.64 us

profile of v5, /device:TPU:1, one launch (start us, length us, event | category | flops | bytes accessed | tf_op | source)
XLA Modules:
  0.0 77.9 jit_solution(3002245135077007969)
XLA Ops:
  0.6 74.5 %sums.1 = (f32[2304,256]{1,0:T(8,128)S(1)}, f32[80,256]{1,0:T(8,128)S(1)}, f32[1,256]{1,0:T(1,128)S(1)}, f32[80,2304]{1,0:T(8,128)S(1)}) custom-call(f32[80,2304]{1,0:T(8,128)} %g_ref.1, f32[80,2304]{1,0:T(8,128)} %m_ref.1, f32[2304,256]{1,0:T(8,128)} %r_ref.1), custom_call_target="tpu_custom_call" | custom-call | tf_op jit(solution)/shard_map/sums/pallas_call | solution.py:476
  75.1 2.6 %outputs.1 = (f32[80,2304]{1,0:T(8,128)}, f32[80,2304]{1,0:T(8,128)}, f32[2304,256]{1,0:T(8,128)}) custom-call(f32[80,2304]{1,0:T(8,128)S(1)} %get-tuple-element.7.b_ref, f32[2304,256]{1,0:T(8,128)S(1)} %get-tuple-element.8.r_ref, f32[80,256]{1,0:T(8,128)S(1)} %get-tuple-element.9.ortho_ref, f32[1,256]{1,0:T(1,128)S(1)} %get-tuple-element.10.inv_ref), custom_call_target="tpu_custom_call" | custom-call | tf_op jit(solution)/shard_map/outputs/pallas_call | solution.py:496
